TPU v7x, 32 devices: a whole 2x2x4 slice. The times are simulated.
32 devices in a mesh: dp: 4 (over z), expert: 8 (over y, x, core).
Axes of the slice: x: 2, y: 2, z: 4, core: 2. Of those that a mesh axis runs over, the one named last changes fastest.
Arguments:
- tokens: bfloat16 [32, 212, 1024], P(('dp', 'expert')), may hold values from -6 to 6
- expert_ids: int32 [32, 212, 1], P(('dp', 'expert')), may hold values from 0 to 7; in each aligned block of 212 rows (0 to 211, 212 to 423, ..., all dimensions but the last counted through in order) at most 36 rows name the same one
- caption_lengths: int32 [32], P(('dp', 'expert')), may hold values from 1 to 16, as said below
- layer_norm_gain: float32 [1024], replicated, may hold values from 0.5 to 1.5
- router: float32 [1024, 8], replicated, may hold values from -0.1875 to 0.1875
- w_up: bfloat16 [8, 1024, 4096], P('expert', None, 'dp'), may hold values from -0.1875 to 0.1875
- w_down: bfloat16 [8, 4096, 1024], P('expert', 'dp'), may hold values from -0.09375 to 0.09375
- logit_scale: float32 [1], replicated, may hold values from 5 to 20
- logit_bias: float32 [1], replicated, may hold values from -4 to -1.5
Outputs:
- loss: float32 [1], replicated
- grad_tokens: bfloat16 [32, 212, 1024], P(('dp', 'expert'))
- grad_up: float32 [8, 1024, 4096], P('expert', None, 'dp')
- grad_down: float32 [8, 4096, 1024], P('expert', 'dp')
- grad_router: float32 [1024, 8], replicated
- layer_gain_gradient: float32 [1024], replicated
Inputs may be any that keep to these rules, and one draw needn't show every extreme that they name: `expert_ids`: among the rows of one device (aligned blocks of 212 rows, devices ordered by dp then expert) no expert is named more than 36 times, a bound that some block reaches. `caption_lengths`: some caption has all 16 tokens.
All inputs are finite; a program needn't handle non-finite values.
Results may differ from a plain program's by a relative error of at most 0.009.
Values may be sent and summed in bfloat16 or wider, within the bound.
A program may use at most 128 MiB of HBM per device.

v0:
```python
import jax
import jax.numpy as jnp
from jax import lax
from jax.sharding import PartitionSpec as P

D = 1024
PATCH = 196
CAPLEN = 16
SEQ = 212
eps = 1e-06
loss_scale = 1024.0


def gelu_slope(pre):
    return (
        0.5 * (1.0 + lax.erf(pre * 0.7071067811865476))
        + pre * jnp.exp(-0.5 * pre * pre) * 0.3989422804014327
    )


def deliver(buffer, experts, slots):
    width = buffer.shape[-1]
    sent = lax.all_to_all(
        buffer.reshape(experts, 1, slots, width), "expert", split_axis=0, concat_axis=1, tiled=True
    )
    shaped = sent.reshape(sent.shape[0], 1, sent.shape[1], slots, width)
    whole = lax.all_gather(shaped, "dp", axis=1, tiled=True)
    return whole.reshape(whole.shape[0], -1, width)


def give_back(partial_value, n_dp, n_expert, slots):
    local = partial_value.shape[0]
    width = partial_value.shape[-1]
    summed = lax.psum_scatter(
        partial_value.reshape(local, n_dp, n_expert * slots, width).astype(jnp.bfloat16),
        "dp",
        scatter_dimension=1,
        tiled=True,
    )
    rounded = summed.reshape(local, n_expert, slots, width)
    returned = lax.all_to_all(rounded, "expert", split_axis=1, concat_axis=0, tiled=True)
    return returned.reshape(-1, width)


def body(
    tokens,
    expert_ids,
    caption_lengths,
    layer_norm_gain,
    router,
    w_up,
    w_down,
    logit_scale,
    logit_bias,
):
    n_dp = lax.axis_size("dp")
    n_expert = lax.axis_size("expert")
    pair_dev = tokens.shape[0]
    rows = pair_dev * SEQ
    experts = router.shape[1]
    slots = rows * 4 // (3 * experts) + 1
    pairs_all = pair_dev * n_dp * n_expert
    input_rows = tokens.reshape(rows, D).astype(jnp.float32)
    input_mean = jnp.mean(input_rows, axis=1, keepdims=True)
    var_x = jnp.mean((input_rows - input_mean) ** 2, axis=1, keepdims=True)
    inverse_deviation = 1.0 / jnp.sqrt(var_x + eps)
    centered_scaled_input = (input_rows - input_mean) * inverse_deviation
    normalized_input = (centered_scaled_input * layer_norm_gain).astype(jnp.bfloat16)
    ids = expert_ids.reshape(rows)
    onehot = (ids[:, None] == jnp.arange(experts, dtype=jnp.int32)[None, :]).astype(jnp.int32)
    slot = jnp.sum((jnp.cumsum(onehot, axis=0) - 1) * onehot, axis=1)
    dest = ids * slots + slot
    onehot_f = onehot.astype(jnp.float32)
    buffer = jnp.zeros((experts * slots, D), jnp.bfloat16).at[dest].set(normalized_input)
    gathered = deliver(buffer, experts, slots)
    pre = jnp.einsum("erd,edf->erf", gathered, w_up, preferred_element_type=jnp.float32)
    act = jax.nn.gelu(pre, approximate=False).astype(jnp.bfloat16)
    partial_value = jnp.einsum("erf,efd->erd", act, w_down, preferred_element_type=jnp.float32)
    moe = give_back(partial_value, n_dp, n_expert, slots)[dest].astype(jnp.float32)
    xnf = normalized_input.astype(jnp.float32)
    router_logits = jnp.dot(xnf, router, precision=lax.Precision.HIGHEST)
    gate = jax.nn.sigmoid(jnp.sum(router_logits * onehot_f, axis=1))
    y = (input_rows + gate[:, None] * moe).reshape(pair_dev, SEQ, D)
    img = jnp.mean(y[:, :PATCH], axis=1)
    lengths = caption_lengths.astype(jnp.float32)
    mask = (jnp.arange(CAPLEN, dtype=jnp.int32)[None, :] < caption_lengths[:, None]).astype(
        jnp.float32
    )
    txt = jnp.sum(y[:, PATCH:] * mask[:, :, None], axis=1) / lengths[:, None]
    ru = jnp.sqrt(jnp.mean(img * img, axis=1, keepdims=True) + eps)
    rv = jnp.sqrt(jnp.mean(txt * txt, axis=1, keepdims=True) + eps)
    u = img / ru
    v = txt / rv
    scale = logit_scale[0]
    first = lax.axis_index(("dp", "expert")) * pair_dev
    mine = first + jnp.arange(pair_dev, dtype=jnp.int32)
    every = jnp.arange(pairs_all, dtype=jnp.int32)
    own_sign = jnp.where(mine[:, None] == every[None, :], 1.0, -1.0)
    u_all, v_all = (
        lax.all_gather(u, ("dp", "expert"), axis=0, tiled=True),
        lax.all_gather(v, ("dp", "expert"), axis=0, tiled=True),
    )
    logits = scale * jnp.dot(u, v_all.T, precision=lax.Precision.HIGHEST) / D + logit_bias[0]
    loss_term = -jnp.sum(jax.nn.log_sigmoid(own_sign * logits)) / pairs_all
    coef = -(loss_scale / pairs_all) * own_sign * jax.nn.sigmoid(-own_sign * logits)
    du = scale / D * jnp.dot(coef, v_all, precision=lax.Precision.HIGHEST)
    column_logits = scale * jnp.dot(u_all, v.T, precision=lax.Precision.HIGHEST) / D + logit_bias[0]
    column_sign = own_sign.T
    column_coef = (
        -(loss_scale / pairs_all) * column_sign * jax.nn.sigmoid(-column_sign * column_logits)
    )
    dv = scale / D * jnp.dot(column_coef.T, u_all, precision=lax.Precision.HIGHEST)
    dimg = (du - u * jnp.mean(du * u, axis=1, keepdims=True)) / ru
    dtxt = (dv - v * jnp.mean(dv * v, axis=1, keepdims=True)) / rv
    dy_img = jnp.broadcast_to(dimg[:, None, :] / PATCH, (pair_dev, PATCH, D))
    dy_txt = (dtxt / lengths[:, None])[:, None, :] * mask[:, :, None]
    dy = jnp.concatenate([dy_img, dy_txt], axis=1).reshape(rows, D)
    dmoe = (gate[:, None] * dy).astype(jnp.bfloat16)
    dgl = jnp.sum(dy * moe, axis=1) * gate * (1.0 - gate)
    router_part = jnp.dot(xnf.T, onehot_f * dgl[:, None], precision=lax.Precision.HIGHEST)
    grad_buffer = jnp.zeros((experts * slots, D), jnp.bfloat16).at[dest].set(dmoe)
    gathered_grads = deliver(grad_buffer, experts, slots)
    dact = jnp.einsum("erd,efd->erf", gathered_grads, w_down, preferred_element_type=jnp.float32)
    dpre = (dact * gelu_slope(pre)).astype(jnp.bfloat16)
    grad_down = jnp.einsum("erf,erd->efd", act, gathered_grads, preferred_element_type=jnp.float32)
    grad_up = jnp.einsum("erd,erf->edf", gathered, dpre, preferred_element_type=jnp.float32)
    back_partial = jnp.einsum("erf,edf->erd", dpre, w_up, preferred_element_type=jnp.float32)
    dxe = give_back(back_partial, n_dp, n_expert, slots)[dest].astype(jnp.float32)
    router_rows = jnp.dot(onehot_f, router.T, precision=lax.Precision.HIGHEST)
    gradient_normalized_input = dxe + dgl[:, None] * router_rows
    gain_partial_term = jnp.sum(gradient_normalized_input * centered_scaled_input, axis=0)
    scaled_output_gradient = gradient_normalized_input * layer_norm_gain
    normed_input_gradient = (
        scaled_output_gradient
        - jnp.mean(scaled_output_gradient, axis=1, keepdims=True)
        - centered_scaled_input
        * jnp.mean(scaled_output_gradient * centered_scaled_input, axis=1, keepdims=True)
    ) * inverse_deviation
    grad_tokens = (dy + normed_input_gradient).astype(jnp.bfloat16).reshape(pair_dev, SEQ, D)
    loss, grad_router, layer_gain_gradient = lax.psum(
        (loss_term, router_part, gain_partial_term), ("dp", "expert")
    )
    return (loss.reshape(1), grad_tokens, grad_up, grad_down, grad_router, layer_gain_gradient)


def solution(mesh):
    return jax.shard_map(
        body,
        mesh=mesh,
        in_specs=(
            P(("dp", "expert"), None, None),
            P(("dp", "expert"), None, None),
            P(("dp", "expert")),
            P(),
            P(),
            P("expert", None, "dp"),
            P("expert", "dp", None),
            P(),
            P(),
        ),
        out_specs=(
            P(),
            P(("dp", "expert"), None, None),
            P("expert", None, "dp"),
            P("expert", "dp", None),
            P(),
            P(),
        ),
        check_vma=False,
    )
```

profile of v0, /device:TPU:0, one launch (start us, length us, event | category | flops | bytes accessed | tf_op | source)
XLA Modules:
  0.0 468.2 jit_solution(15633228378693927035)
XLA Ops:
  15.3 16.1 %all_to_all.16 = bf16[8,1,36,1024]{3,2,1,0:T(8,128)(2,1)S(1)} all-to-all(bf16[8,1,36,1024]{3,2,1,0:T(8,128)(2,1)S(1)} %bitcast.185), channel_id=1, replica_groups=mesh['dp'=4,'expert'=8] {'expert'}, dimensions={0} | all-to-all | bytes 1179648 | tf_op jit(solution)/shard_map/all_to_all | solution.py:23
  32.6 49.5 %all-gather.7.cloned.1.call-done = bf16[32,1,36,1024]{3,0,2,1:T(8,128)(2,1)} async-done(((bf16[8,1,36,1024]{3,0,2,1:T(8,128)(2,1)}), bf16[32,1,36,1024]{3,0,2,1:T(8,128)(2,1)}) %all-gather.7.cloned.1.call-update) | async-done | bytes 2359312 | tf_op jit(solution)/shard_map/all_gather | solution.py:27
  82.1 4.5 copy.17
  86.5 4.1 reshape.516
  90.7 14.6 %fusion.2 = (bf16[1152,1024]{1,0:T(8,128)(2,1)S(1)}, f32[1152,1024]{1,0:T(8,128)}) fusion(bf16[1152,1024]{1,0:T(8,128)(2,1)} %reshape.516, bf16[1,1024,1024]{2,1,0:T(8,128)(2,1)S(1)} %copy-done), kind=kOutput, calls=%fused_computation.9 | convolution fusion | flops 2492596224 | bytes 11534336 | tf_op jit(solution)/shard_map/erd,edf->erf/dot_general | solution.py:76
  106.7 3.8 convert_bitcast_fusion.1
  111.5 45.7 %reduce-scatter.3.cloned.1.call-done = bf16[1,1,288,1024]{3,2,1,0:T(8,128)(2,1)} async-done(((bf16[1,4,288,1024]{3,2,1,0:T(8,128)(2,1)}), bf16[1,1,288,1024]{3,2,1,0:T(8,128)(2,1)}) %reduce-scatter.3.cloned.1.call-update) | async-done | bytes 589840 | tf_op jit(solution)/shard_map/reduce_scatter | solution.py:34
  159.2 4.2 all-to-all-start.1
  165.3 9.2 %all-to-all-done.1 = bf16[1,8,36,1024]{3,2,0,1:T(8,128)(2,1)} async-done(((bf16[1,8,36,1024]{3,2,0,1:T(8,128)(2,1)}), bf16[1,8,36,1024]{3,2,0,1:T(8,128)(2,1)}, u32[]{:S(2)}, u32[]{:S(2)}) %all-to-all-start.1) | async-done | bytes 589856 | tf_op jit(solution)/shard_map/all_to_all | solution.py:41
  181.6 38.6 %all-gather.1 = f32[32768]{0:T(1024)S(1)} all-gather(f32[1024]{0:T(1024)S(1)} %broadcast_divide_fusion), channel_id=3, replica_groups=mesh['dp'=4,'expert'=8] {'dp','expert'}, dimensions={0}, use_global_device_ids=true | all-gather | bytes 135168 | tf_op jit(solution)/shard_map/all_gather | solution.py:101
  220.2 37.2 %all-gather.2 = f32[32768]{0:T(1024)S(1)} all-gather(f32[1024]{0:T(1024)S(1)} %multiply_divide_fusion), channel_id=4, replica_groups=mesh['dp'=4,'expert'=8] {'dp','expert'}, dimensions={0}, use_global_device_ids=true | all-gather | bytes 135168 | tf_op jit(solution)/shard_map/all_gather | solution.py:100
  266.0 14.6 %all_to_all.17 = bf16[8,1,36,1024]{3,2,1,0:T(8,128)(2,1)S(1)} all-to-all(bf16[8,1,36,1024]{3,2,1,0:T(8,128)(2,1)} %bitcast.186), channel_id=1, replica_groups=mesh['dp'=4,'expert'=8] {'expert'}, dimensions={0} | all-to-all | bytes 1179648 | tf_op jit(solution)/shard_map/all_to_all | solution.py:23
  281.8 46.4 %all-gather.9.cloned.1.call-done = bf16[32,1,36,1024]{3,0,2,1:T(8,128)(2,1)} async-done(((bf16[8,1,36,1024]{3,0,2,1:T(8,128)(2,1)}), bf16[32,1,36,1024]{3,0,2,1:T(8,128)(2,1)}) %all-gather.9.cloned.1.call-update) | async-done | bytes 2359312 | tf_op jit(solution)/shard_map/all_gather | solution.py:27
  328.2 4.5 copy.21
  332.7 4.1 reshape.525
  336.8 6.8 %fusion.14 = bf16[1152,1024]{1,0:T(8,128)(2,1)S(1)} fusion(f32[1152,1024]{1,0:T(8,128)} %get-tuple-element.13, bf16[1152,1024]{1,0:T(8,128)(2,1)} %reshape.525, bf16[1,1024,1024]{2,1,0:T(8,128)(2,1)} %param.15), kind=kOutput, calls=%fused_computation.29 | convolution fusion | flops 2427715584 | bytes 11534336 | tf_op jit(solution)/shard_map/erd,efd->erf/dot_general | solution.py:123
  345.0 3.9 convert_bitcast_fusion
  352.2 7.7 %convolution_bitcast_fusion = f32[1,1024,1024]{2,1,0:T(8,128)} fusion(bf16[1152,1024]{1,0:T(8,128)(2,1)} %copy-done.8, bf16[1152,1024]{1,0:T(8,128)(2,1)} %reshape.525), kind=kOutput, calls=%fused_computation.32 | convolution fusion | flops 2415919104 | bytes 8912896 | tf_op jit(solution)/shard_map/erf,erd->efd/dot_general | solution.py:125
  359.9 35.7 %reduce-scatter.5.cloned.1.call-done = bf16[1,1,288,1024]{3,2,1,0:T(8,128)(2,1)} async-done(((bf16[1,4,288,1024]{3,2,1,0:T(8,128)(2,1)}), bf16[1,1,288,1024]{3,2,1,0:T(8,128)(2,1)}) %reduce-scatter.5.cloned.1.call-update) | async-done | bytes 589840 | tf_op jit(solution)/shard_map/reduce_scatter | solution.py:34
  397.6 4.4 all-to-all-start.3
  402.0 7.3 %convolution_bitcast_fusion.1 = f32[1,1024,1024]{2,1,0:T(8,128)} fusion(bf16[1152,1024]{1,0:T(8,128)(2,1)} %reshape.516, bf16[1152,1024]{1,0:T(8,128)(2,1)} %copy-done.9), kind=kOutput, calls=%fused_computation.33 | convolution fusion | flops 2415919104 | bytes 8912896 | tf_op jit(solution)/shard_map/erd,erf->edf/dot_general | solution.py:126
  409.4 3.6 all-to-all-done.3
  416.0 3.1 fusion.56
  419.1 40.1 %all-reduce.1 = (f32[1]{0:T(128)}, f32[1024,8]{0,1:T(8,128)}, f32[1024]{0:T(1024)}) all-reduce(f32[1]{0:T(128)} %bitcast.22, f32[1024,8]{0,1:T(8,128)S(1)} %fusion.70, f32[1024]{0:T(1024)S(1)} %get-tuple-element.6), channel_id=1, replica_groups=mesh['dp'=4,'expert'=8] {'dp','expert'}, use_global_device_ids=true, to_apply=%region_13.14 | all-reduce | flops 9217 | bytes 73736 | tf_op jit(solution)/shard_map/psum | solution.py:140
  (82 shorter events, 39.1 us)
Async XLA Ops:
  7.2 83.5 %copy-start = (bf16[1,1024,1024]{2,1,0:T(8,128)(2,1)S(1)}, bf16[1,1024,1024]{2,1,0:T(8,128)(2,1)}, u32[]{:S(2)}) copy-start(bf16[1,1024,1024]{2,1,0:T(8,128)(2,1)} %param.14) | copy-start | bytes 6291460
  7.2 74.9 %all-gather.7.cloned.1.call-start = ((), (), s32[]{:S(2)}) async-start(), calls=%async_computation.8 | async-start | bytes 2949120 | tf_op jit(solution)/shard_map/all_gather | solution.py:27
  32.6 124.7 %reduce-scatter.3.cloned.1.call-start = ((), (), s32[]{:S(2)}) async-start(), calls=%async_computation.6 | async-start | bytes 2949120 | tf_op jit(solution)/shard_map/reduce_scatter | solution.py:34
  90.6 16.1 %copy-start.7 = (bf16[1,1024,1024]{2,1,0:T(8,128)(2,1)S(1)}, bf16[1,1024,1024]{2,1,0:T(8,128)(2,1)}, u32[]{:S(2)}) copy-start(bf16[1,1024,1024]{2,1,0:T(8,128)(2,1)} %param.15) | copy-start | bytes 6291460
  105.3 1.5 copy-start.8
  106.7 4.5 copy-start.1
  106.7 4.5 copy-start.4
  110.6 54.3 %copy-start.5 = (f32[1024,8]{0,1:T(8,128)S(1)}, f32[1024,8]{0,1:T(8,128)}, u32[]{:S(2)}) copy-start(f32[1024,8]{0,1:T(8,128)} %param.13) | copy-start | bytes 98308
  110.6 54.3 %copy-start.6 = (s32[1,212,1]{1,2,0:T(1,128)S(1)}, s32[1,212,1]{1,2,0:T(1,128)}, u32[]{:S(2)}) copy-start(s32[1,212,1]{1,2,0:T(1,128)} %param.10) | copy-start | bytes 2548
  111.5 53.8 %copy-start.3 = (bf16[212,1024]{1,0:T(8,128)(2,1)}, bf16[212,1024]{1,0:T(8,128)(2,1)S(1)}, u32[]{:S(2)}) copy-start(bf16[212,1024]{1,0:T(8,128)(2,1)S(1)} %fusion.50) | copy-start | bytes 1302532
  159.2 15.3 %all-to-all-start.1 = ((bf16[1,8,36,1024]{3,2,0,1:T(8,128)(2,1)}), bf16[1,8,36,1024]{3,2,0,1:T(8,128)(2,1)}, u32[]{:S(2)}, u32[]{:S(2)}) async-start(bf16[1,8,36,1024]{3,2,0,1:T(8,128)(2,1)} %bitcast.184), calls=%async_computation.2 | async-start | bytes 1310720 | tf_op jit(solution)/shard_map/all_to_all | solution.py:41
  163.4 164.8 %all-gather.9.cloned.1.call-start = ((), (), s32[]{:S(2)}) async-start(), calls=%async_computation.9 | async-start | bytes 2949120 | tf_op jit(solution)/shard_map/all_gather | solution.py:27
  261.6 88.0 %copy-start.2 = (f32[1,196,1024]{2,1,0:T(8,128)}, f32[1,196,1024]{2,1,0:T(8,128)S(1)}, u32[]{:S(2)}) copy-start(f32[1,196,1024]{2,1,0:T(8,128)S(1)} %broadcast_in_dim.10) | copy-start | bytes 2408452
  281.8 113.9 %reduce-scatter.5.cloned.1.call-start = ((), (), s32[]{:S(2)}) async-start(), calls=%async_computation.7 | async-start | bytes 2949120 | tf_op jit(solution)/shard_map/reduce_scatter | solution.py:34
  343.6 1.4 copy-start.9
  397.6 15.3 %all-to-all-start.3 = ((bf16[1,8,36,1024]{3,2,0,1:T(8,128)(2,1)}), bf16[1,8,36,1024]{3,2,0,1:T(8,128)(2,1)}, u32[]{:S(2)}, u32[]{:S(2)}) async-start(bf16[1,8,36,1024]{3,2,0,1:T(8,128)(2,1)} %bitcast.34), calls=%async_computation.5 | async-start | bytes 1310720 | tf_op jit(solution)/shard_map/all_to_all | solution.py:41
Sparse Core Ops, SparseCore 0:
  32.7 49.3 all-gather.6
  110.7 46.4 reduce-scatter.2
  281.9 46.2 all-gather.8
  349.1 46.4 reduce-scatter.4
where the time goes:
time: 470 us; the launch traced here: 468 us
  waiting for transfers between devices  190 us (40%)
  blocking collectives  147 us (31%)
  matrix products  50.6 us (11%)
  local copies, waits for them, and re-layouts  34.9 us (7%)
  between operations  19.4 us (4%)
  other arithmetic  18 us (4%)
  starting transfers between devices  8.79 us (2%)
    all_gather x2, waiting for transfers between devices, deliver(): whole = lax.all_gather(shaped, 'dp', axis=1, tiled=True)  95.9 us
    reduce_scatter x2, waiting for transfers between devices, give_back(): lax.psum_scatter(partial_value.reshape(local, n_dp, n_expert * slots, wid...  81.4 us
    psum x1, blocking collectives, body(): lax.psum((loss_term, router_part, gain_partial_term), ('dp', 'expert'))  40.1 us
    all_gather x1, blocking collectives, body(): lax.all_gather(v, ('dp', 'expert'), axis=0, tiled=True)  38.6 us
    all_gather x1, blocking collectives, body(): lax.all_gather(u, ('dp', 'expert'), axis=0, tiled=True)  37.2 us
    all_to_all x2, blocking collectives, deliver(): lax.all_to_all(buffer.reshape(experts, 1, slots, width), 'expert', split_...  30.7 us
    dot_general x1, matrix products, body(): jnp.einsum('erd,edf->erf', gathered, w_up, preferred_element_type=jnp.flo...  14.6 us
    all_to_all x2, waiting for transfers between devices, give_back(): lax.all_to_all(rounded, 'expert', split_axis=1, concat_axis=0, tiled=True)  12.8 us
  transfers between devices with their start and end apart: 6, of which 6 were waited for; matrix products, arithmetic and copies ran while one was open for 4% of the time, Pallas kernels for 0%

commit v1 on v0

--- a/solution.py
+++ b/solution.py
@@ -97,7 +97,12 @@
     every = jnp.arange(pairs_all, dtype=jnp.int32)
     own_sign = jnp.where(mine[:, None] == every[None, :], 1.0, -1.0)
     u_all, v_all = (
-        lax.all_gather(u, ("dp", "expert"), axis=0, tiled=True),
+        jnp.concatenate(
+            lax.all_to_all(
+                jnp.stack([u] * lax.axis_size(("dp", "expert"))), ("dp", "expert"), 0, 0
+            ),
+            axis=0,
+        ),
         lax.all_gather(v, ("dp", "expert"), axis=0, tiled=True),
     )
     logits = scale * jnp.dot(u, v_all.T, precision=lax.Precision.HIGHEST) / D + logit_bias[0]

time: 470 us -> 445 us (0.947)
  blocking collectives: 147 us -> 109 us
  waiting for transfers between devices: 190 us -> 198 us
    all_gather x1 -> x0, blocking collectives: 37.2 us -> none  [body(): lax.all_gather(u, ('dp', 'expert'), axis=0, tiled=True)]
    all_to_all x0 -> x1, waiting for transfers between devices: none -> 6.88 us  [body(): lax.all_to_all(jnp.stack([u] * lax.axis_size(('dp', 'expert'))), ('dp', '...]
  transfers between devices with their start and end apart: 6 -> 7, of which waited for: 6 -> 7; matrix products, arithmetic and copies ran while one was open for 4% -> 4% of each run, Pallas kernels for 0% -> 0%
where the time goes in v1:
time: 445 us; the launch traced here: 444 us
  waiting for transfers between devices  198 us (44%)
  blocking collectives  109 us (24%)
  matrix products  50.6 us (11%)
  local copies, waits for them, and re-layouts  36.6 us (8%)
  between operations  19.3 us (4%)
  other arithmetic  18.6 us (4%)
  starting transfers between devices  11.4 us (3%)
    all_gather x2, waiting for transfers between devices, deliver(): whole = lax.all_gather(shaped, 'dp', axis=1, tiled=True)  96.6 us
    reduce_scatter x2, waiting for transfers between devices, give_back(): lax.psum_scatter(partial_value.reshape(local, n_dp, n_expert * slots, wid...  81.4 us
    psum x1, blocking collectives, body(): lax.psum((loss_term, router_part, gain_partial_term), ('dp', 'expert'))  40.1 us
    all_gather x1, blocking collectives, body(): lax.all_gather(v, ('dp', 'expert'), axis=0, tiled=True)  38.8 us
    all_to_all x2, blocking collectives, deliver(): lax.all_to_all(buffer.reshape(experts, 1, slots, width), 'expert', split_...  30.7 us
    dot_general x1, matrix products, body(): jnp.einsum('erd,edf->erf', gathered, w_up, preferred_element_type=jnp.flo...  14.6 us
    all_to_all x2, waiting for transfers between devices, give_back(): lax.all_to_all(rounded, 'expert', split_axis=1, concat_axis=0, tiled=True)  12.9 us
    all_gather x2, local copies, waits for them, and re-layouts, deliver(): whole = lax.all_gather(shaped, 'dp', axis=1, tiled=True)  8.94 us
  transfers between devices with their start and end apart: 7, of which 7 were waited for; matrix products, arithmetic and copies ran while one was open for 4% of the time, Pallas kernels for 0%

profile of v1, /device:TPU:0, one launch (start us, length us, event | category | flops | bytes accessed | tf_op | source)
XLA Modules:
  0.0 443.8 jit_solution(13328622317405310590)
XLA Ops:
  17.0 16.1 %all_to_all.20 = bf16[8,1,36,1024]{3,2,1,0:T(8,128)(2,1)S(1)} all-to-all(bf16[8,1,36,1024]{3,2,1,0:T(8,128)(2,1)S(1)} %bitcast.188), channel_id=1, replica_groups=mesh['dp'=4,'expert'=8] {'expert'}, dimensions={0} | all-to-all | bytes 1179648 | tf_op jit(solution)/shard_map/all_to_all | solution.py:23
  34.3 49.5 %all-gather.6.cloned.1.call-done = bf16[32,1,36,1024]{3,0,2,1:T(8,128)(2,1)} async-done(((bf16[8,1,36,1024]{3,0,2,1:T(8,128)(2,1)}), bf16[32,1,36,1024]{3,0,2,1:T(8,128)(2,1)}) %all-gather.6.cloned.1.call-update) | async-done | bytes 2359312 | tf_op jit(solution)/shard_map/all_gather | solution.py:27
  83.8 4.5 %copy.17 = bf16[32,1,36,1024]{3,2,0,1:T(8,128)(2,1)} copy(bf16[32,1,36,1024]{3,0,2,1:T(8,128)(2,1)} %all-gather.6.cloned.1.call-done) | data formatting | bytes 4718592 | tf_op jit(solution)/shard_map/all_gather | solution.py:27
  88.2 4.1 reshape.512
  92.4 14.6 %fusion.2 = (bf16[1152,1024]{1,0:T(8,128)(2,1)S(1)}, f32[1152,1024]{1,0:T(8,128)}) fusion(bf16[1152,1024]{1,0:T(8,128)(2,1)} %reshape.512, bf16[1,1024,1024]{2,1,0:T(8,128)(2,1)S(1)} %copy-done), kind=kOutput, calls=%fused_computation.9 | convolution fusion | flops 2492596224 | bytes 11534336 | tf_op jit(solution)/shard_map/erd,edf->erf/dot_general | solution.py:76
  108.4 3.8 convert_bitcast_fusion.1
  113.2 45.7 %reduce-scatter.3.cloned.1.call-done = bf16[1,1,288,1024]{3,2,1,0:T(8,128)(2,1)} async-done(((bf16[1,4,288,1024]{3,2,1,0:T(8,128)(2,1)}), bf16[1,1,288,1024]{3,2,1,0:T(8,128)(2,1)}) %reduce-scatter.3.cloned.1.call-update) | async-done | bytes 589840 | tf_op jit(solution)/shard_map/reduce_scatter | solution.py:34
  160.9 4.2 all-to-all-start.1
  167.0 9.3 %all-to-all-done.1 = bf16[1,8,36,1024]{3,2,0,1:T(8,128)(2,1)} async-done(((bf16[1,8,36,1024]{3,2,0,1:T(8,128)(2,1)}), bf16[1,8,36,1024]{3,2,0,1:T(8,128)(2,1)}, u32[]{:S(2)}, u32[]{:S(2)}) %all-to-all-start.1) | async-done | bytes 589856 | tf_op jit(solution)/shard_map/all_to_all | solution.py:41
  183.3 38.8 %all-gather.1 = f32[32768]{0:T(1024)S(1)} all-gather(f32[1024]{0:T(1024)S(1)} %broadcast_divide_fusion), channel_id=3, replica_groups=mesh['dp'=4,'expert'=8] {'dp','expert'}, dimensions={0}, use_global_device_ids=true | all-gather | bytes 135168 | tf_op jit(solution)/shard_map/all_gather | solution.py:106
  227.8 6.9 %all-to-all-done.2 = f32[32,1,1024]{2,1,0:T(1,128)S(1)} async-done(((f32[32,1,1024]{2,1,0:T(1,128)}), f32[32,1,1024]{2,1,0:T(1,128)S(1)}, u32[]{:S(2)}, u32[]{:S(2)}) %all-to-all-start.2) | async-done | bytes 131104 | tf_op jit(solution)/shard_map/all_to_all | solution.py:101
  240.9 14.6 %all_to_all.42 = bf16[8,1,36,1024]{3,2,1,0:T(8,128)(2,1)S(1)} all-to-all(bf16[8,1,36,1024]{3,2,1,0:T(8,128)(2,1)} %bitcast.189), channel_id=1, replica_groups=mesh['dp'=4,'expert'=8] {'expert'}, dimensions={0} | all-to-all | bytes 1179648 | tf_op jit(solution)/shard_map/all_to_all | solution.py:23
  256.7 47.1 %all-gather.8.cloned.1.call-done = bf16[32,1,36,1024]{3,0,2,1:T(8,128)(2,1)} async-done(((bf16[8,1,36,1024]{3,0,2,1:T(8,128)(2,1)}), bf16[32,1,36,1024]{3,0,2,1:T(8,128)(2,1)}) %all-gather.8.cloned.1.call-update) | async-done | bytes 2359312 | tf_op jit(solution)/shard_map/all_gather | solution.py:27
  303.8 4.5 %copy.21 = bf16[32,1,36,1024]{3,2,0,1:T(8,128)(2,1)} copy(bf16[32,1,36,1024]{3,0,2,1:T(8,128)(2,1)} %all-gather.8.cloned.1.call-done) | data formatting | bytes 4718592 | tf_op jit(solution)/shard_map/all_gather | solution.py:27
  308.3 4.1 reshape.522
  312.4 6.8 %fusion.14 = bf16[1152,1024]{1,0:T(8,128)(2,1)S(1)} fusion(f32[1152,1024]{1,0:T(8,128)} %get-tuple-element.13, bf16[1152,1024]{1,0:T(8,128)(2,1)} %reshape.522, bf16[1,1024,1024]{2,1,0:T(8,128)(2,1)} %param.15), kind=kOutput, calls=%fused_computation.29 | convolution fusion | flops 2427715584 | bytes 11534336 | tf_op jit(solution)/shard_map/erd,efd->erf/dot_general | solution.py:128
  320.6 3.9 convert_bitcast_fusion
  327.8 7.7 %convolution_bitcast_fusion = f32[1,1024,1024]{2,1,0:T(8,128)} fusion(bf16[1152,1024]{1,0:T(8,128)(2,1)} %copy-done.8, bf16[1152,1024]{1,0:T(8,128)(2,1)} %reshape.522), kind=kOutput, calls=%fused_computation.32 | convolution fusion | flops 2415919104 | bytes 8912896 | tf_op jit(solution)/shard_map/erf,erd->efd/dot_general | solution.py:130
  335.5 35.7 %reduce-scatter.5.cloned.1.call-done = bf16[1,1,288,1024]{3,2,1,0:T(8,128)(2,1)} async-done(((bf16[1,4,288,1024]{3,2,1,0:T(8,128)(2,1)}), bf16[1,1,288,1024]{3,2,1,0:T(8,128)(2,1)}) %reduce-scatter.5.cloned.1.call-update) | async-done | bytes 589840 | tf_op jit(solution)/shard_map/reduce_scatter | solution.py:34
  373.2 4.4 all-to-all-start.4
  377.7 7.3 %convolution_bitcast_fusion.1 = f32[1,1024,1024]{2,1,0:T(8,128)} fusion(bf16[1152,1024]{1,0:T(8,128)(2,1)} %reshape.512, bf16[1152,1024]{1,0:T(8,128)(2,1)} %copy-done.9), kind=kOutput, calls=%fused_computation.33 | convolution fusion | flops 2415919104 | bytes 8912896 | tf_op jit(solution)/shard_map/erd,erf->edf/dot_general | solution.py:131
  385.0 3.6 all-to-all-done.4
  391.6 3.1 fusion.56
  394.7 40.1 %all-reduce.1 = (f32[1]{0:T(128)}, f32[1024,8]{0,1:T(8,128)}, f32[1024]{0:T(1024)}) all-reduce(f32[1]{0:T(128)} %bitcast.22, f32[1024,8]{0,1:T(8,128)S(1)} %fusion.75, f32[1024]{0:T(1024)S(1)} %get-tuple-element.6), channel_id=1, replica_groups=mesh['dp'=4,'expert'=8] {'dp','expert'}, use_global_device_ids=true, to_apply=%region_13.14 | all-reduce | flops 9217 | bytes 73736 | tf_op jit(solution)/shard_map/psum | solution.py:145
  (83 shorter events, 44.1 us)
Async XLA Ops:
  7.2 85.2 %copy-start = (bf16[1,1024,1024]{2,1,0:T(8,128)(2,1)S(1)}, bf16[1,1024,1024]{2,1,0:T(8,128)(2,1)}, u32[]{:S(2)}) copy-start(bf16[1,1024,1024]{2,1,0:T(8,128)(2,1)} %param.14) | copy-start | bytes 6291460
  7.2 76.6 %all-gather.6.cloned.1.call-start = ((), (), s32[]{:S(2)}) async-start(), calls=%async_computation.9 | async-start | bytes 2949120 | tf_op jit(solution)/shard_map/all_gather | solution.py:27
  34.3 124.7 %reduce-scatter.3.cloned.1.call-start = ((), (), s32[]{:S(2)}) async-start(), calls=%async_computation.7 | async-start | bytes 2949120 | tf_op jit(solution)/shard_map/reduce_scatter | solution.py:34
  92.4 16.1 %copy-start.7 = (bf16[1,1024,1024]{2,1,0:T(8,128)(2,1)S(1)}, bf16[1,1024,1024]{2,1,0:T(8,128)(2,1)}, u32[]{:S(2)}) copy-start(bf16[1,1024,1024]{2,1,0:T(8,128)(2,1)} %param.15) | copy-start | bytes 6291460
  107.0 1.5 copy-start.8
  108.4 4.5 %copy-start.1 = (bf16[1,212,1024]{2,1,0:T(8,128)(2,1)S(1)}, bf16[1,212,1024]{2,1,0:T(8,128)(2,1)}, u32[]{:S(2)}) copy-start(bf16[1,212,1024]{2,1,0:T(8,128)(2,1)} %param.9) | copy-start | bytes 1302532
  108.4 4.5 %copy-start.4 = (f32[1024]{0:T(1024)S(1)}, f32[1024]{0:T(1024)}, u32[]{:S(2)}) copy-start(f32[1024]{0:T(1024)} %param.12) | copy-start | bytes 12292
  112.3 54.2 %copy-start.5 = (f32[1024,8]{0,1:T(8,128)S(1)}, f32[1024,8]{0,1:T(8,128)}, u32[]{:S(2)}) copy-start(f32[1024,8]{0,1:T(8,128)} %param.13) | copy-start | bytes 98308
  112.3 54.2 %copy-start.6 = (s32[1,212,1]{1,2,0:T(1,128)S(1)}, s32[1,212,1]{1,2,0:T(1,128)}, u32[]{:S(2)}) copy-start(s32[1,212,1]{1,2,0:T(1,128)} %param.10) | copy-start | bytes 2548
  113.2 53.8 %copy-start.3 = (bf16[212,1024]{1,0:T(8,128)(2,1)}, bf16[212,1024]{1,0:T(8,128)(2,1)S(1)}, u32[]{:S(2)}) copy-start(bf16[212,1024]{1,0:T(8,128)(2,1)S(1)} %fusion.50) | copy-start | bytes 1302532
  160.9 15.3 %all-to-all-start.1 = ((bf16[1,8,36,1024]{3,2,0,1:T(8,128)(2,1)}), bf16[1,8,36,1024]{3,2,0,1:T(8,128)(2,1)}, u32[]{:S(2)}, u32[]{:S(2)}) async-start(bf16[1,8,36,1024]{3,2,0,1:T(8,128)(2,1)} %bitcast.187), calls=%async_computation.2 | async-start | bytes 1310720 | tf_op jit(solution)/shard_map/all_to_all | solution.py:41
  223.8 10.8 %all-to-all-start.2 = ((f32[32,1,1024]{2,1,0:T(1,128)}), f32[32,1,1024]{2,1,0:T(1,128)S(1)}, u32[]{:S(2)}, u32[]{:S(2)}) async-start(f32[32,1,1024]{2,1,0:T(1,128)} %stack.2), calls=%async_computation.3 | async-start | bytes 262144 | tf_op jit(solution)/shard_map/all_to_all | solution.py:101
  226.4 77.4 %all-gather.8.cloned.1.call-start = ((), (), s32[]{:S(2)}) async-start(), calls=%async_computation.10 | async-start | bytes 2949120 | tf_op jit(solution)/shard_map/all_gather | solution.py:27
  236.5 88.7 %copy-start.2 = (f32[1,196,1024]{2,1,0:T(8,128)}, f32[1,196,1024]{2,1,0:T(8,128)S(1)}, u32[]{:S(2)}) copy-start(f32[1,196,1024]{2,1,0:T(8,128)S(1)} %broadcast_in_dim.10) | copy-start | bytes 2408452
  256.7 114.6 %reduce-scatter.5.cloned.1.call-start = ((), (), s32[]{:S(2)}) async-start(), calls=%async_computation.8 | async-start | bytes 2949120 | tf_op jit(solution)/shard_map/reduce_scatter | solution.py:34
  319.2 1.4 copy-start.9
  373.2 15.3 %all-to-all-start.4 = ((bf16[1,8,36,1024]{3,2,0,1:T(8,128)(2,1)}), bf16[1,8,36,1024]{3,2,0,1:T(8,128)(2,1)}, u32[]{:S(2)}, u32[]{:S(2)}) async-start(bf16[1,8,36,1024]{3,2,0,1:T(8,128)(2,1)} %bitcast.34), calls=%async_computation.6 | async-start | bytes 1310720 | tf_op jit(solution)/shard_map/all_to_all | solution.py:41
Sparse Core Ops, SparseCore 0:
  34.4 49.3 all-gather.5
  112.4 46.4 reduce-scatter.2
  256.8 46.9 all-gather.7
  324.7 46.4 reduce-scatter.4
